TPU v7x, 32 devices: a whole 2x2x4 slice. The times are simulated.
32 devices in a mesh: dp: 8 (over z, y), tensor: 4 (over x, core).
Axes of the slice: x: 2, y: 2, z: 4, core: 2. Of those that a mesh axis runs over, the one named last changes fastest.
Arguments:
- block_input: bfloat16 [2, 1024, 8, 1024], P(None, 'tensor', 'dp'), may hold values from -6 to 6
- qkv_weight: bfloat16 [1024, 3, 1024], P('dp', None, 'tensor'), may hold values from -0.1875 to 0.1875
- qv_bias: float32 [2, 1024], P(None, 'tensor'), may hold values from -2 to 2
- out_weight: bfloat16 [1024, 1024], P('dp', 'tensor'), may hold values from -0.75 to 0.75
- out_bias: float32 [1024], replicated, may hold values from -2 to 2
- fc_weight: bfloat16 [1024, 4096], P('dp', 'tensor'), may hold values from -0.1875 to 0.1875
- fc_bias: float32 [4096], P('tensor'), may hold values from -2 to 2
- proj_weight: bfloat16 [1024, 4096], P('dp', 'tensor'), may hold values from -0.09375 to 0.09375
- proj_bias: float32 [1024], replicated, may hold values from -2 to 2
- norm1_gain: float32 [1024], replicated, may hold values from 0.1 to 1.9
- norm1_shift: float32 [1024], replicated, may hold values from -2 to 2
- norm2_gain: float32 [1024], replicated, may hold values from 0.1 to 1.9
- norm2_shift: float32 [1024], replicated, may hold values from -2 to 2
- out_grad: bfloat16 [2, 1024, 8, 1024], P(None, 'tensor', 'dp'), may hold values from -6 to 6
Outputs:
- block_output: bfloat16 [2, 1024, 8, 1024], P(None, 'tensor', 'dp')
- input_grad: bfloat16 [2, 1024, 8, 1024], P(None, 'tensor', 'dp')
- qkv_weight_grad: float32 [1024, 3, 1024], P('dp', None, 'tensor')
- qv_bias_grad: float32 [2, 1024], P(None, 'tensor')
- out_weight_grad: float32 [1024, 1024], P('dp', 'tensor')
- out_bias_grad: float32 [1024], replicated
- fc_weight_grad: float32 [1024, 4096], P('dp', 'tensor')
- fc_bias_grad: float32 [4096], P('tensor')
- proj_weight_grad: float32 [1024, 4096], P('dp', 'tensor')
- proj_bias_grad: float32 [1024], replicated
- norm1_gain_grad: float32 [1024], replicated
- norm1_shift_grad: float32 [1024], replicated
- norm2_gain_grad: float32 [1024], replicated
- norm2_shift_grad: float32 [1024], replicated
All inputs are finite; a program needn't handle non-finite values.
Results may differ from a plain program's by a relative error of at most 0.012.
Values may be sent and summed in bfloat16 or wider, within the bound.
A program may use at most 128 MiB of HBM per device.

v0:
```python
import jax
import jax.numpy as jnp
from jax import lax
from jax.sharding import PartitionSpec as P

HEAD_DIM = 64
norm_eps = 1e-05
tanh_coef = 0.7978845608028654
cube_coef = 0.044715
block_rows = 512


def gelu_tanh(values):
    return (
        0.5 * values * (1.0 + jnp.tanh(tanh_coef * (values + cube_coef * values * values * values)))
    )


def norm_parts(rows):
    center = rows - jnp.mean(rows, axis=-1, keepdims=True)
    spread = jnp.mean(center * center, axis=-1, keepdims=True)
    inverse = lax.rsqrt(spread + norm_eps)
    return (center * inverse, inverse)


def norm_back(grad_out, normed, inverse, gain):
    grad_normed = grad_out * gain
    first = jnp.mean(grad_normed, axis=-1, keepdims=True)
    second = jnp.mean(grad_normed * normed, axis=-1, keepdims=True)
    return inverse * (grad_normed - first - normed * second)


def causal_scores(query_block, keys, offset):
    scores = jnp.einsum(
        "qbhe,kbhe->bhqk", query_block, keys, preferred_element_type=jnp.float32
    ) * HEAD_DIM ** (-0.5)
    height = query_block.shape[0]
    length = keys.shape[0]
    row_pos = lax.broadcasted_iota(jnp.int32, (height, length), 0) + offset
    col_pos = lax.broadcasted_iota(jnp.int32, (height, length), 1)
    return jnp.where(col_pos <= row_pos, scores, -1e30)


def attend_forward(queries, keys, values):
    length = keys.shape[0]
    span = min(block_rows, length)
    outputs = []
    totals = []
    for offset in range(0, length, span):
        scores = causal_scores(queries[offset : offset + span], keys, offset)
        peak = jnp.max(scores, axis=-1, keepdims=True)
        raised = jnp.exp(scores - peak)
        total = jnp.sum(raised, axis=-1, keepdims=True)
        weights = (raised / total).astype(jnp.bfloat16)
        outputs.append(
            jnp.einsum("bhqk,kbhe->qbhe", weights, values, preferred_element_type=jnp.float32)
        )
        totals.append(peak + jnp.log(total))
    return (jnp.concatenate(outputs, 0), jnp.concatenate(totals, 2))


def attend_backward(queries, keys, values, log_totals, grad_out):
    length = keys.shape[0]
    span = min(block_rows, length)
    scale = HEAD_DIM ** (-0.5)
    grad_queries = []
    grad_keys = jnp.zeros(keys.shape, jnp.float32)
    grad_values = jnp.zeros(values.shape, jnp.float32)
    for offset in range(0, length, span):
        query_block = queries[offset : offset + span]
        grad_block = grad_out[offset : offset + span]
        scores = causal_scores(query_block, keys, offset)
        probs = jnp.exp(scores - log_totals[:, :, offset : offset + span])
        grad_probs = jnp.einsum(
            "qbhe,kbhe->bhqk", grad_block, values, preferred_element_type=jnp.float32
        )
        inner = jnp.sum(probs * grad_probs, axis=-1, keepdims=True)
        grad_scores = (probs * (grad_probs - inner)).astype(jnp.bfloat16)
        grad_queries.append(
            jnp.einsum("bhqk,kbhe->qbhe", grad_scores, keys, preferred_element_type=jnp.float32)
            * scale
        )
        grad_keys = (
            grad_keys
            + jnp.einsum(
                "bhqk,qbhe->kbhe", grad_scores, query_block, preferred_element_type=jnp.float32
            )
            * scale
        )
        grad_values = grad_values + jnp.einsum(
            "bhqk,qbhe->kbhe",
            probs.astype(jnp.bfloat16),
            grad_block,
            preferred_element_type=jnp.float32,
        )
    return (jnp.concatenate(grad_queries, 0), grad_keys, grad_values)


def per_device(
    block_input,
    qkv_weight,
    qv_bias,
    out_weight,
    out_bias,
    fc_weight,
    fc_bias,
    proj_weight,
    proj_bias,
    norm1_gain,
    norm1_shift,
    norm2_gain,
    norm2_shift,
    out_grad,
):
    micro = block_input.shape[0]
    heads_local = qkv_weight.shape[2] // HEAD_DIM
    rows = qkv_weight.shape[0]
    width_qkv = qkv_weight.shape[1] * qkv_weight.shape[2]
    width_out = out_weight.shape[1]
    width_fc = fc_weight.shape[1]
    cuts = (width_qkv, width_qkv + width_out, width_qkv + width_out + width_fc)
    packed = jnp.concatenate(
        [qkv_weight.reshape(rows, width_qkv), out_weight, fc_weight, proj_weight], axis=1
    )
    packed_full = lax.all_gather(packed, "dp", axis=0, tiled=True)
    depth = packed_full.shape[0]
    qkv_full = packed_full[:, : cuts[0]].reshape(depth, 3, qkv_weight.shape[2])
    out_full = packed_full[:, cuts[0] : cuts[1]]
    fc_full = packed_full[:, cuts[1] : cuts[2]]
    proj_full = packed_full[:, cuts[2] :]
    grad_top_all = lax.all_gather(out_grad, "tensor", axis=1, tiled=True)
    weight_init = jnp.zeros(packed_full.shape, jnp.float32)
    small_init = (
        jnp.zeros(qv_bias.shape, jnp.float32),
        jnp.zeros(fc_bias.shape, jnp.float32),
        jnp.zeros(out_bias.shape, jnp.float32),
        jnp.zeros(proj_bias.shape, jnp.float32),
        jnp.zeros(norm1_gain.shape, jnp.float32),
        jnp.zeros(norm1_shift.shape, jnp.float32),
        jnp.zeros(norm2_gain.shape, jnp.float32),
        jnp.zeros(norm2_shift.shape, jnp.float32),
    )
    outputs_init = jnp.zeros(block_input.shape, jnp.bfloat16)
    in_grads_init = jnp.zeros(block_input.shape, jnp.bfloat16)

    def one_micro(index, carry):
        outputs_all, in_grads_all, weight_acc, small_acc = carry
        resid_in = lax.dynamic_index_in_dim(block_input, index, 0, keepdims=False).astype(
            jnp.float32
        )
        grad_top = lax.dynamic_index_in_dim(out_grad, index, 0, keepdims=False)
        grad_top_full = lax.dynamic_index_in_dim(grad_top_all, index, 0, keepdims=False)
        normed1, inverse1 = norm_parts(resid_in)
        hidden1 = (normed1 * norm1_gain + norm1_shift).astype(jnp.bfloat16)
        hidden1_full = lax.all_gather(hidden1, "tensor", axis=0, tiled=True)
        length = hidden1_full.shape[0]
        batch = hidden1_full.shape[1]
        projected = jnp.einsum(
            "lbd,dce->lbce", hidden1_full, qkv_full, preferred_element_type=jnp.float32
        )
        qkv_bias = jnp.stack([qv_bias[0], jnp.zeros_like(qv_bias[0]), qv_bias[1]])
        qkv_values = (projected + qkv_bias).astype(jnp.bfloat16)
        split = qkv_values.reshape(length, batch, 3, heads_local, HEAD_DIM)
        queries = split[:, :, 0]
        keys = split[:, :, 1]
        values = split[:, :, 2]
        attended, log_totals = attend_forward(queries, keys, values)
        mixed = attended.astype(jnp.bfloat16).reshape(length, batch, heads_local * HEAD_DIM)
        attn_branch = lax.psum_scatter(
            jnp.einsum("lbi,oi->lbo", mixed, out_full, preferred_element_type=jnp.float32),
            "tensor",
            scatter_dimension=0,
            tiled=True,
        )
        middle = resid_in + attn_branch + out_bias
        normed2, inverse2 = norm_parts(middle)
        hidden2 = (normed2 * norm2_gain + norm2_shift).astype(jnp.bfloat16)
        hidden2_full = lax.all_gather(hidden2, "tensor", axis=0, tiled=True)
        pre_act = (
            jnp.einsum("lbd,df->lbf", hidden2_full, fc_full, preferred_element_type=jnp.float32)
            + fc_bias
        )
        activated = gelu_tanh(pre_act).astype(jnp.bfloat16)
        mlp_branch = lax.psum_scatter(
            jnp.einsum(
                "lbf,of->lbo", activated, proj_full, preferred_element_type=jnp.float32
            ).astype(jnp.bfloat16),
            "tensor",
            scatter_dimension=0,
            tiled=True,
        ).astype(jnp.float32)
        block_out = (middle + mlp_branch + proj_bias).astype(jnp.bfloat16)
        grad_proj = jnp.einsum(
            "lbo,lbf->of", grad_top_full, activated, preferred_element_type=jnp.float32
        )
        grad_act = jnp.einsum(
            "lbo,of->lbf", grad_top_full, proj_full, preferred_element_type=jnp.float32
        )
        _, gelu_pull = jax.vjp(gelu_tanh, pre_act)
        grad_pre = gelu_pull(grad_act)[0].astype(jnp.bfloat16)
        grad_fc_bias = jnp.sum(grad_pre.astype(jnp.float32), axis=(0, 1))
        grad_fc = jnp.einsum(
            "lbd,lbf->df", hidden2_full, grad_pre, preferred_element_type=jnp.float32
        )
        grad_h2 = lax.psum_scatter(
            jnp.einsum("lbf,df->lbd", grad_pre, fc_full, preferred_element_type=jnp.float32),
            "tensor",
            scatter_dimension=0,
            tiled=True,
        )
        grad_gain2 = jnp.sum(grad_h2 * normed2, axis=(0, 1))
        grad_shift2 = jnp.sum(grad_h2, axis=(0, 1))
        grad_mid = grad_top.astype(jnp.float32) + norm_back(grad_h2, normed2, inverse2, norm2_gain)
        grad_out_bias = jnp.sum(grad_mid, axis=(0, 1))
        grad_proj_bias = jnp.sum(grad_top.astype(jnp.float32), axis=(0, 1))
        grad_mid_full = lax.all_gather(grad_mid.astype(jnp.bfloat16), "tensor", axis=0, tiled=True)
        grad_out_w = jnp.einsum(
            "lbo,lbi->oi", grad_mid_full, mixed, preferred_element_type=jnp.float32
        )
        grad_mixed = jnp.einsum(
            "lbo,oi->lbi", grad_mid_full, out_full, preferred_element_type=jnp.float32
        )
        grad_mixed = grad_mixed.astype(jnp.bfloat16).reshape(length, batch, heads_local, HEAD_DIM)
        grad_queries, grad_keys, grad_values = attend_backward(
            queries, keys, values, log_totals, grad_mixed
        )
        grad_qkv = jnp.stack([grad_queries, grad_keys, grad_values], axis=2).astype(jnp.bfloat16)
        grad_qkv = grad_qkv.reshape(length, batch, 3, heads_local * HEAD_DIM)
        kind_sums = jnp.sum(grad_qkv.astype(jnp.float32), axis=(0, 1))
        grad_qv_bias = jnp.stack([kind_sums[0], kind_sums[2]])
        grad_qkv_w = jnp.einsum(
            "lbd,lbce->dce", hidden1_full, grad_qkv, preferred_element_type=jnp.float32
        )
        grad_h1 = lax.psum_scatter(
            jnp.einsum("lbce,dce->lbd", grad_qkv, qkv_full, preferred_element_type=jnp.float32),
            "tensor",
            scatter_dimension=0,
            tiled=True,
        )
        grad_gain1 = jnp.sum(grad_h1 * normed1, axis=(0, 1))
        grad_shift1 = jnp.sum(grad_h1, axis=(0, 1))
        grad_in = (grad_mid + norm_back(grad_h1, normed1, inverse1, norm1_gain)).astype(
            jnp.bfloat16
        )
        fresh_weights = jnp.concatenate(
            [grad_qkv_w.reshape(depth, width_qkv), grad_out_w, grad_fc, grad_proj], axis=1
        )
        weight_acc = weight_acc + fresh_weights
        fresh = (
            grad_qv_bias,
            grad_fc_bias,
            grad_out_bias,
            grad_proj_bias,
            grad_gain1,
            grad_shift1,
            grad_gain2,
            grad_shift2,
        )
        small_acc = tuple((total + extra for total, extra in zip(small_acc, fresh)))
        outputs_all = lax.dynamic_update_index_in_dim(outputs_all, block_out, index, 0)
        in_grads_all = lax.dynamic_update_index_in_dim(in_grads_all, grad_in, index, 0)
        return (outputs_all, in_grads_all, weight_acc, small_acc)

    outputs_all, in_grads_all, weight_acc, small_acc = lax.fori_loop(
        0, micro, one_micro, (outputs_init, in_grads_init, weight_init, small_init)
    )
    weight_shard = lax.psum_scatter(weight_acc, "dp", scatter_dimension=0, tiled=True)
    grad_qkv_w = weight_shard[:, : cuts[0]].reshape(qkv_weight.shape)
    grad_out_w = weight_shard[:, cuts[0] : cuts[1]]
    grad_fc_w = weight_shard[:, cuts[1] : cuts[2]]
    grad_proj_w = weight_shard[:, cuts[2] :]
    tensor_size = lax.psum(1, "tensor")
    slot = lax.axis_index("tensor")
    head_vec = jnp.concatenate([small_acc[0].reshape(-1), small_acc[1]])
    head_slots = jnp.zeros((tensor_size, head_vec.shape[0]), jnp.float32)
    head_slots = lax.dynamic_update_index_in_dim(head_slots, head_vec, slot, 0)
    feature_vec = jnp.concatenate([item for item in small_acc[2:]])
    total = lax.psum(jnp.concatenate([feature_vec, head_slots.reshape(-1)]), ("dp", "tensor"))
    features = total[: feature_vec.shape[0]].reshape(6, -1)
    head_total = lax.dynamic_index_in_dim(
        total[feature_vec.shape[0] :].reshape(tensor_size, -1), slot, 0, keepdims=False
    )
    qv_size = small_acc[0].size
    grad_qv_bias = head_total[:qv_size].reshape(small_acc[0].shape)
    grad_fc_bias = head_total[qv_size:]
    return (
        outputs_all,
        in_grads_all,
        grad_qkv_w,
        grad_qv_bias,
        grad_out_w,
        features[0],
        grad_fc_w,
        grad_fc_bias,
        grad_proj_w,
        features[1],
        features[2],
        features[3],
        features[4],
        features[5],
    )


def solution(mesh):
    in_specs = (
        P(None, "tensor", "dp", None),
        P("dp", None, "tensor"),
        P(None, "tensor"),
        P("dp", "tensor"),
        P(),
        P("dp", "tensor"),
        P("tensor"),
        P("dp", "tensor"),
        P(),
        P(),
        P(),
        P(),
        P(),
        P(None, "tensor", "dp", None),
    )
    out_specs = (
        P(None, "tensor", "dp", None),
        P(None, "tensor", "dp", None),
        P("dp", None, "tensor"),
        P(None, "tensor"),
        P("dp", "tensor"),
        P(),
        P("dp", "tensor"),
        P("tensor"),
        P("dp", "tensor"),
        P(),
        P(),
        P(),
        P(),
        P(),
    )
    return jax.shard_map(
        per_device, mesh=mesh, in_specs=in_specs, out_specs=out_specs, check_vma=False
    )
```

profile of v0, /device:TPU:0, one launch (start us, length us, event | category | flops | bytes accessed | tf_op | source)
XLA Modules:
  0.0 999.4 jit_solution(10423390227295797122)
XLA Ops:
  13.4 101.5 %all-gather.6.cloned.1.call-done = bf16[1024,3072]{0,1:T(8,128)(2,1)} async-done(((bf16[128,3072]{0,1:T(8,128)(2,1)}), bf16[1024,3072]{0,1:T(8,128)(2,1)}) %all-gather.6.cloned.1.call-update) | async-done | bytes 6291472 | tf_op jit(solution)/shard_map/all_gather | solution.py:125
  130.1 19.0 %all-gather.8.cloned.1.call-done = bf16[2,1024,1,1024]{3,1,2,0:T(8,128)(2,1)} async-done(((bf16[2,256,1,1024]{3,1,2,0:T(8,128)(2,1)}), bf16[2,1024,1,1024]{3,1,2,0:T(8,128)(2,1)}) %all-gather.8.cloned.1.call-update) | async-done | bytes 4194320 | tf_op jit(solution)/shard_map/all_gather | solution.py:131
  149.1 623.7 %while.34 = (s32[]{:T(128)}, bf16[2,256,1,1024]{3,1,2,0:T(8,128)(2,1)}, bf16[2,256,1,1024]{3,1,2,0:T(8,128)(2,1)}, f32[1024,3072]{0,1:T(8,128)}, f32[2,256]{1,0:...) while((s32[]{:T(128)}, ...), condition=%wide.region_27.28_spmd.clone, body=%wide.region_0.27_spmd.clone.sunk | while | flops 22718711808 | bytes 744419392 | solution.py:264
  151.7 23.2 %all-gather.10.cloned.1.call-done = bf16[1024,1,1024]{2,0,1:T(8,128)(2,1)} async-done(((bf16[256,1,1024]{2,0,1:T(8,128)(2,1)}), bf16[1024,1,1024]{2,0,1:T(8,128)(2,1)}) %all-gather.10.cloned.1.call-update) | async-done | bytes 2097168 | tf_op jit(solution)/shard_map/while/body/eval_jaxpr/all_gather | solution.py:155
  196.7 44.7 %reduce-scatter.8.cloned.1.call-done = f32[256,1,1024]{2,0,1:T(8,128)} async-done(((f32[1024,1,1024]{2,0,1:T(8,128)}), f32[256,1,1024]{2,0,1:T(8,128)}) %reduce-scatter.8.cloned.1.call-update) | async-done | bytes 1048592 | tf_op jit(solution)/shard_map/while/body/eval_jaxpr/reduce_scatter | solution.py:169
  244.5 22.4 %all-gather.12.cloned.1.call-done = bf16[1024,1,1024]{2,0,1:T(8,128)(2,1)} async-done(((bf16[256,1,1024]{2,0,1:T(8,128)(2,1)}), bf16[1024,1,1024]{2,0,1:T(8,128)(2,1)}) %all-gather.12.cloned.1.call-update) | async-done | bytes 2097168 | tf_op jit(solution)/shard_map/while/body/eval_jaxpr/all_gather | solution.py:178
  283.1 44.7 %reduce-scatter.12.cloned.1.call-done = f32[256,1,1024]{2,0,1:T(8,128)} async-done(((f32[1024,1,1024]{2,0,1:T(8,128)}), f32[256,1,1024]{2,0,1:T(8,128)}) %reduce-scatter.12.cloned.1.call-update) | async-done | bytes 1048592 | tf_op jit(solution)/shard_map/while/body/eval_jaxpr/reduce_scatter | solution.py:205
  332.3 7.0 convert_bitcast_fusion.4
  339.8 15.1 %all-gather.14.cloned.1.call-done = bf16[1024,1,1024]{2,0,1:T(8,128)(2,1)} async-done(((bf16[256,1,1024]{2,0,1:T(8,128)(2,1)}), bf16[1024,1,1024]{2,0,1:T(8,128)(2,1)}) %all-gather.14.cloned.1.call-update) | async-done | bytes 2097168 | tf_op jit(solution)/shard_map/while/body/eval_jaxpr/all_gather | solution.py:216
  362.4 7.6 multiply_reduce_fusion.13
  374.6 6.8 multiply_convert_fusion.11
  444.2 11.6 %reduce-scatter.14.cloned.1.call-done = f32[256,1,1024]{2,0,1:T(8,128)} async-done(((f32[1024,1,1024]{2,0,1:T(8,128)}), f32[256,1,1024]{2,0,1:T(8,128)}) %reduce-scatter.14.cloned.1.call-update) | async-done | bytes 1048592 | tf_op jit(solution)/shard_map/while/body/eval_jaxpr/reduce_scatter | solution.py:234
  462.6 22.9 %all-gather.10.cloned.1.call-done = bf16[1024,1,1024]{2,0,1:T(8,128)(2,1)} async-done(((bf16[256,1,1024]{2,0,1:T(8,128)(2,1)}), bf16[1024,1,1024]{2,0,1:T(8,128)(2,1)}) %all-gather.10.cloned.1.call-update) | async-done | bytes 2097168 | tf_op jit(solution)/shard_map/while/body/eval_jaxpr/all_gather | solution.py:155
  507.3 44.7 %reduce-scatter.8.cloned.1.call-done = f32[256,1,1024]{2,0,1:T(8,128)} async-done(((f32[1024,1,1024]{2,0,1:T(8,128)}), f32[256,1,1024]{2,0,1:T(8,128)}) %reduce-scatter.8.cloned.1.call-update) | async-done | bytes 1048592 | tf_op jit(solution)/shard_map/while/body/eval_jaxpr/reduce_scatter | solution.py:169
  555.3 22.2 %all-gather.12.cloned.1.call-done = bf16[1024,1,1024]{2,0,1:T(8,128)(2,1)} async-done(((bf16[256,1,1024]{2,0,1:T(8,128)(2,1)}), bf16[1024,1,1024]{2,0,1:T(8,128)(2,1)}) %all-gather.12.cloned.1.call-update) | async-done | bytes 2097168 | tf_op jit(solution)/shard_map/while/body/eval_jaxpr/all_gather | solution.py:178
  593.7 44.7 %reduce-scatter.12.cloned.1.call-done = f32[256,1,1024]{2,0,1:T(8,128)} async-done(((f32[1024,1,1024]{2,0,1:T(8,128)}), f32[256,1,1024]{2,0,1:T(8,128)}) %reduce-scatter.12.cloned.1.call-update) | async-done | bytes 1048592 | tf_op jit(solution)/shard_map/while/body/eval_jaxpr/reduce_scatter | solution.py:205
  642.9 7.0 convert_bitcast_fusion.4
  650.1 15.4 %all-gather.14.cloned.1.call-done = bf16[1024,1,1024]{2,0,1:T(8,128)(2,1)} async-done(((bf16[256,1,1024]{2,0,1:T(8,128)(2,1)}), bf16[1024,1,1024]{2,0,1:T(8,128)(2,1)}) %all-gather.14.cloned.1.call-update) | async-done | bytes 2097168 | tf_op jit(solution)/shard_map/while/body/eval_jaxpr/all_gather | solution.py:216
  673.0 7.6 multiply_reduce_fusion.13
  685.1 6.8 multiply_convert_fusion.11
  749.2 10.1 %maximum_add_fusion.4 = f32[1024,3072]{0,1:T(8,128)} fusion(f32[1024,1024]{0,1:T(8,128)S(1)} %copy-done.11, f32[1024,1024]{0,1:T(8,128)S(1)} %copy-done.10, f32[1024,256]{0,1:T(8,128)S(1)} %fusion.228, f32[1024,768]{0,1:T(8,128)S(1)} %fusion.230, f32[1024,3072]{0,1:T(8,128)} %get-tuple-element.947, pred[]{:T(512)S(6)} %compare.3), kind=kLoop, calls=%fused_computation.clone.1 | loop fusion | flops 15728640 | bytes 37748736 | tf_op jit(solution)/shard_map/while/body/eval_jaxpr/add | solution.py:248
  759.3 7.1 reduce-scatter.14.cloned.1.call-done
  773.7 43.1 %psum.7 = f32[12288]{0:T(1024)S(1)} all-reduce(f32[12288]{0:T(1024)S(1)} %constant_dynamic-update-slice_fusion), channel_id=1, replica_groups=mesh['dp'=8,'tensor'=4] {'dp','tensor'}, use_global_device_ids=true, to_apply=%region_29.30 | all-reduce | flops 12288 | bytes 98304 | tf_op jit(solution)/shard_map/psum | solution.py:278
  818.7 167.7 %reduce-scatter.6.cloned.1.call-done = f32[128,3072]{0,1:T(8,128)} async-done(((f32[1024,3072]{0,1:T(8,128)}), f32[128,3072]{0,1:T(8,128)}) %reduce-scatter.6.cloned.1.call-update) | async-done | bytes 1572880 | tf_op jit(solution)/shard_map/reduce_scatter | solution.py:267
  (362 shorter events, 277.8 us)
Async XLA Ops:
  7.2 107.7 %all-gather.6.cloned.1.call-start = ((), (), s32[]{:S(2)}) async-start(), calls=%async_computation.5 | async-start | bytes 7077888 | tf_op jit(solution)/shard_map/all_gather | solution.py:125
  12.5 136.6 %all-gather.8.cloned.1.call-start = ((), (), s32[]{:S(2)}) async-start(), calls=%async_computation.6 | async-start | bytes 5242880 | tf_op jit(solution)/shard_map/all_gather | solution.py:131
  122.7 26.3 %copy-start.5 = (bf16[2,256,1,1024]{3,1,2,0:T(8,128)(2,1)S(1)}, bf16[2,256,1,1024]{3,1,2,0:T(8,128)(2,1)}, u32[]{:S(2)}) copy-start(bf16[2,256,1,1024]{3,1,2,0:T(8,128)(2,1)} %param.16) | copy-start | bytes 3145732
  122.7 26.3 %copy-start.20 = (f32[1024]{0:T(1024)S(1)}, f32[1024]{0:T(1024)}, u32[]{:S(2)}) copy-start(f32[1024]{0:T(1024)} %param.25) | copy-start | bytes 12292
  122.7 26.3 %copy-start.21 = (f32[1024]{0:T(1024)S(1)}, f32[1024]{0:T(1024)}, u32[]{:S(2)}) copy-start(f32[1024]{0:T(1024)} %param.27) | copy-start | bytes 12292
  122.7 26.3 %copy-start.22 = (f32[1024]{0:T(1024)S(1)}, f32[1024]{0:T(1024)}, u32[]{:S(2)}) copy-start(f32[1024]{0:T(1024)} %param.26) | copy-start | bytes 12292
  122.8 26.3 %copy-start.23 = (f32[1024]{0:T(1024)S(1)}, f32[1024]{0:T(1024)}, u32[]{:S(2)}) copy-start(f32[1024]{0:T(1024)} %param.20) | copy-start | bytes 12292
  149.4 43.9 %copy-start.16 = (bf16[1024,256]{1,0:T(8,128)(2,1)}, bf16[1024,256]{1,0:T(8,128)(2,1)S(1)}, u32[]{:S(2)}) copy-start(bf16[1024,256]{1,0:T(8,128)(2,1)S(1)} %get-tuple-element.992) | copy-start | bytes 1572868 | tf_op jit(solution)/shard_map/while
  149.4 25.5 %all-gather.10.cloned.1.call-start = ((), (), s32[]{:S(2)}) async-start(), calls=%async_computation.8 | async-start | bytes 2621440 | tf_op jit(solution)/shard_map/while/body/eval_jaxpr/all_gather | solution.py:155
  151.0 90.4 %reduce-scatter.8.cloned.1.call-start = ((), (), s32[]{:S(2)}) async-start(), calls=%async_computation.9 | async-start | bytes 5242880 | tf_op jit(solution)/shard_map/while/body/eval_jaxpr/reduce_scatter | solution.py:169
  196.6 70.3 %all-gather.12.cloned.1.call-start = ((), (), s32[]{:S(2)}) async-start(), calls=%async_computation.10 | async-start | bytes 2621440 | tf_op jit(solution)/shard_map/while/body/eval_jaxpr/all_gather | solution.py:178
  244.1 83.6 %reduce-scatter.12.cloned.1.call-start = ((), (), s32[]{:S(2)}) async-start(), calls=%async_computation.12 | async-start | bytes 5242880 | tf_op jit(solution)/shard_map/while/body/eval_jaxpr/reduce_scatter | solution.py:205
  283.0 71.9 %all-gather.14.cloned.1.call-start = ((), (), s32[]{:S(2)}) async-start(), calls=%async_computation.13 | async-start | bytes 2621440 | tf_op jit(solution)/shard_map/while/body/eval_jaxpr/all_gather | solution.py:216
  332.2 91.3 %reduce-scatter.10.cloned.1.call-start = ((), (), s32[]{:S(2)}) async-start(), calls=%async_computation.11 | async-start | bytes 2621440 | tf_op jit(solution)/shard_map/while/body/eval_jaxpr/reduce_scatter | solution.py:184
  339.3 116.5 %reduce-scatter.14.cloned.1.call-start = ((), (), s32[]{:S(2)}) async-start(), calls=%async_computation.14 | async-start | bytes 5242880 | tf_op jit(solution)/shard_map/while/body/eval_jaxpr/reduce_scatter | solution.py:234
  460.3 43.6 %copy-start.16 = (bf16[1024,256]{1,0:T(8,128)(2,1)}, bf16[1024,256]{1,0:T(8,128)(2,1)S(1)}, u32[]{:S(2)}) copy-start(bf16[1024,256]{1,0:T(8,128)(2,1)S(1)} %get-tuple-element.992) | copy-start | bytes 1572868 | tf_op jit(solution)/shard_map/while
  460.3 25.2 %all-gather.10.cloned.1.call-start = ((), (), s32[]{:S(2)}) async-start(), calls=%async_computation.8 | async-start | bytes 2621440 | tf_op jit(solution)/shard_map/while/body/eval_jaxpr/all_gather | solution.py:155
  461.9 90.1 %reduce-scatter.8.cloned.1.call-start = ((), (), s32[]{:S(2)}) async-start(), calls=%async_computation.9 | async-start | bytes 5242880 | tf_op jit(solution)/shard_map/while/body/eval_jaxpr/reduce_scatter | solution.py:169
  507.2 70.3 %all-gather.12.cloned.1.call-start = ((), (), s32[]{:S(2)}) async-start(), calls=%async_computation.10 | async-start | bytes 2621440 | tf_op jit(solution)/shard_map/while/body/eval_jaxpr/all_gather | solution.py:178
  554.8 83.6 %reduce-scatter.12.cloned.1.call-start = ((), (), s32[]{:S(2)}) async-start(), calls=%async_computation.12 | async-start | bytes 5242880 | tf_op jit(solution)/shard_map/while/body/eval_jaxpr/reduce_scatter | solution.py:205
  593.6 71.9 %all-gather.14.cloned.1.call-start = ((), (), s32[]{:S(2)}) async-start(), calls=%async_computation.13 | async-start | bytes 2621440 | tf_op jit(solution)/shard_map/while/body/eval_jaxpr/all_gather | solution.py:216
  642.8 91.3 %reduce-scatter.10.cloned.1.call-start = ((), (), s32[]{:S(2)}) async-start(), calls=%async_computation.11 | async-start | bytes 2621440 | tf_op jit(solution)/shard_map/while/body/eval_jaxpr/reduce_scatter | solution.py:184
  649.9 116.5 %reduce-scatter.14.cloned.1.call-start = ((), (), s32[]{:S(2)}) async-start(), calls=%async_computation.14 | async-start | bytes 5242880 | tf_op jit(solution)/shard_map/while/body/eval_jaxpr/reduce_scatter | solution.py:234
  772.8 213.5 %reduce-scatter.6.cloned.1.call-start = ((), (), s32[]{:S(2)}) async-start(), calls=%async_computation.7 | async-start | bytes 14155776 | tf_op jit(solution)/shard_map/reduce_scatter | solution.py:267
  (62 other events, 424.8 us)
Sparse Core Ops, SparseCore 0:
  12.6 102.1 all-gather.5
  116.4 32.6 all-gather.7
  152.3 22.5 all-gather.9
  196.7 44.5 reduce-scatter.7
  244.3 22.5 all-gather.11
  283.1 44.5 reduce-scatter.11
  332.3 22.5 all-gather.13
  357.4 31.1 reduce-scatter.9
  410.9 44.8 reduce-scatter.13
  462.9 22.5 all-gather.9
  507.3 44.5 reduce-scatter.7
  554.9 22.5 all-gather.11
  593.7 44.5 reduce-scatter.11
  642.9 22.5 all-gather.13
  667.9 31.1 reduce-scatter.9
  721.5 44.8 reduce-scatter.13
  776.9 209.3 reduce-scatter.5
where the time goes:
time: 1000 us; the launch traced here: 999 us
  waiting for transfers between devices  608 us (61%)
  matrix products  180 us (18%)
  other arithmetic  85.3 us (9%)
  local copies, waits for them, and re-layouts  62.5 us (6%)
  blocking collectives  43.1 us (4%)
  between operations  14.7 us (1%)
    reduce_scatter x1, waiting for transfers between devices, per_device(): lax.psum_scatter(weight_acc, 'dp', scatter_dimension=0, tiled=True)  168 us
    all_gather x1, waiting for transfers between devices, per_device(): packed_full = lax.all_gather(packed, 'dp', axis=0, tiled=True)  101 us
    reduce_scatter x2, waiting for transfers between devices, one_micro(): lax.psum_scatter(jnp.einsum('lbi,oi->lbo', mixed, out_full, preferred_ele...  89.4 us
    reduce_scatter x2, waiting for transfers between devices, one_micro(): lax.psum_scatter(jnp.einsum('lbf,df->lbd', grad_pre, fc_full, preferred_e...  89.3 us
    all_gather x2, waiting for transfers between devices, one_micro(): hidden1_full = lax.all_gather(hidden1, 'tensor', axis=0, tiled=True)  46.1 us
    all_gather x2, waiting for transfers between devices, one_micro(): hidden2_full = lax.all_gather(hidden2, 'tensor', axis=0, tiled=True)  44.6 us
    psum x1, blocking collectives, per_device(): lax.psum(jnp.concatenate([feature_vec, head_slots.reshape(-1)]), ('dp', '...  43.1 us
    all_gather x2, waiting for transfers between devices, one_micro(): lax.all_gather(grad_mid.astype(jnp.bfloat16), 'tensor', axis=0, tiled=True)  30.5 us
  transfers between devices with their start and end apart: 17, of which 15 were waited for; matrix products, arithmetic and copies ran while one was open for 21% of the time, Pallas kernels for 0%

commit v1 on v0

--- a/solution.py
+++ b/solution.py
@@ -275,7 +275,10 @@
     head_slots = jnp.zeros((tensor_size, head_vec.shape[0]), jnp.float32)
     head_slots = lax.dynamic_update_index_in_dim(head_slots, head_vec, slot, 0)
     feature_vec = jnp.concatenate([item for item in small_acc[2:]])
-    total = lax.psum(jnp.concatenate([feature_vec, head_slots.reshape(-1)]), ("dp", "tensor"))
+    total = jnp.sum(
+        lax.all_gather(jnp.concatenate([feature_vec, head_slots.reshape(-1)]), ("dp", "tensor")),
+        axis=0,
+    )
     features = total[: feature_vec.shape[0]].reshape(6, -1)
     head_total = lax.dynamic_index_in_dim(
         total[feature_vec.shape[0] :].reshape(tensor_size, -1), slot, 0, keepdims=False

time: 1000 us -> 1060 us (1.060)
  waiting for transfers between devices: 608 us -> 704 us
  blocking collectives: 43.1 us -> 0 us
    all_gather x0 -> x1, waiting for transfers between devices: none -> 57.3 us  [per_device(): lax.all_gather(jnp.concatenate([feature_vec, head_slots.reshape(-1)]), ('...]
    psum x1 -> x0, blocking collectives: 43.1 us -> none  [per_device(): lax.psum(jnp.concatenate([feature_vec, head_slots.reshape(-1)]), ('dp', '...]
    reduce_scatter x1, waiting for transfers between devices: 168 us -> 207 us  [per_device(): lax.psum_scatter(weight_acc, 'dp', scatter_dimension=0, tiled=True)]
  transfers between devices with their start and end apart: 17 -> 18, of which waited for: 15 -> 16; matrix products, arithmetic and copies ran while one was open for 21% -> 20% of each run, Pallas kernels for 0% -> 0%
where the time goes in v1:
time: 1060 us
  waiting for transfers between devices  704 us (66%)
  matrix products  180 us (17%)
  other arithmetic  85.4 us (8%)
  local copies, waits for them, and re-layouts  64.8 us (6%)
  between operations  15 us (1%)
    reduce_scatter x1, waiting for transfers between devices, per_device(): lax.psum_scatter(weight_acc, 'dp', scatter_dimension=0, tiled=True)  207 us
    all_gather x1, waiting for transfers between devices, per_device(): packed_full = lax.all_gather(packed, 'dp', axis=0, tiled=True)  101 us
    reduce_scatter x2, waiting for transfers between devices, one_micro(): lax.psum_scatter(jnp.einsum('lbi,oi->lbo', mixed, out_full, preferred_ele...  89.4 us
    reduce_scatter x2, waiting for transfers between devices, one_micro(): lax.psum_scatter(jnp.einsum('lbf,df->lbd', grad_pre, fc_full, preferred_e...  89.3 us
    all_gather x1, waiting for transfers between devices, per_device(): lax.all_gather(jnp.concatenate([feature_vec, head_slots.reshape(-1)]), ('...  57.3 us
    all_gather x2, waiting for transfers between devices, one_micro(): hidden1_full = lax.all_gather(hidden1, 'tensor', axis=0, tiled=True)  46.1 us
    all_gather x2, waiting for transfers between devices, one_micro(): hidden2_full = lax.all_gather(hidden2, 'tensor', axis=0, tiled=True)  44.6 us
    all_gather x2, waiting for transfers between devices, one_micro(): lax.all_gather(grad_mid.astype(jnp.bfloat16), 'tensor', axis=0, tiled=True)  30.4 us
  transfers between devices with their start and end apart: 18, of which 16 were waited for; matrix products, arithmetic and copies ran while one was open for 20% of the time, Pallas kernels for 0%

profile of v1, /device:TPU:0, one launch (start us, length us, event | category | flops | bytes accessed | tf_op | source)
XLA Modules:
  0.0 1055.1 jit_solution(13253355546455531042)
XLA Ops:
  13.4 101.5 %all-gather.8.cloned.1.call-done = bf16[1024,3072]{0,1:T(8,128)(2,1)} async-done(((bf16[128,3072]{0,1:T(8,128)(2,1)}), bf16[1024,3072]{0,1:T(8,128)(2,1)}) %all-gather.8.cloned.1.call-update) | async-done | bytes 6291472 | tf_op jit(solution)/shard_map/all_gather | solution.py:125
  130.1 19.0 %all-gather.10.cloned.1.call-done = bf16[2,1024,1,1024]{3,1,2,0:T(8,128)(2,1)} async-done(((bf16[2,256,1,1024]{3,1,2,0:T(8,128)(2,1)}), bf16[2,1024,1,1024]{3,1,2,0:T(8,128)(2,1)}) %all-gather.10.cloned.1.call-update) | async-done | bytes 4194320 | tf_op jit(solution)/shard_map/all_gather | solution.py:131
  149.2 623.5 %while.34 = (s32[]{:T(128)}, bf16[2,256,1,1024]{3,1,2,0:T(8,128)(2,1)}, bf16[2,256,1,1024]{3,1,2,0:T(8,128)(2,1)}, f32[1024,3072]{0,1:T(8,128)}, f32[2,256]{1,0:...) while((s32[]{:T(128)}, ...), condition=%wide.region_27.28_spmd.clone, body=%wide.region_0.27_spmd.clone.sunk | while | flops 22718711808 | bytes 744419392 | solution.py:264
  151.7 23.2 %all-gather.14.cloned.1.call-done = bf16[1024,1,1024]{2,0,1:T(8,128)(2,1)} async-done(((bf16[256,1,1024]{2,0,1:T(8,128)(2,1)}), bf16[1024,1,1024]{2,0,1:T(8,128)(2,1)}) %all-gather.14.cloned.1.call-update) | async-done | bytes 2097168 | tf_op jit(solution)/shard_map/while/body/eval_jaxpr/all_gather | solution.py:155
  196.7 44.7 %reduce-scatter.8.cloned.1.call-done = f32[256,1,1024]{2,0,1:T(8,128)} async-done(((f32[1024,1,1024]{2,0,1:T(8,128)}), f32[256,1,1024]{2,0,1:T(8,128)}) %reduce-scatter.8.cloned.1.call-update) | async-done | bytes 1048592 | tf_op jit(solution)/shard_map/while/body/eval_jaxpr/reduce_scatter | solution.py:169
  244.5 22.4 %all-gather.16.cloned.1.call-done = bf16[1024,1,1024]{2,0,1:T(8,128)(2,1)} async-done(((bf16[256,1,1024]{2,0,1:T(8,128)(2,1)}), bf16[1024,1,1024]{2,0,1:T(8,128)(2,1)}) %all-gather.16.cloned.1.call-update) | async-done | bytes 2097168 | tf_op jit(solution)/shard_map/while/body/eval_jaxpr/all_gather | solution.py:178
  283.1 44.7 %reduce-scatter.12.cloned.1.call-done = f32[256,1,1024]{2,0,1:T(8,128)} async-done(((f32[1024,1,1024]{2,0,1:T(8,128)}), f32[256,1,1024]{2,0,1:T(8,128)}) %reduce-scatter.12.cloned.1.call-update) | async-done | bytes 1048592 | tf_op jit(solution)/shard_map/while/body/eval_jaxpr/reduce_scatter | solution.py:205
  332.3 7.0 convert_bitcast_fusion.4
  339.9 15.1 %all-gather.18.cloned.1.call-done = bf16[1024,1,1024]{2,0,1:T(8,128)(2,1)} async-done(((bf16[256,1,1024]{2,0,1:T(8,128)(2,1)}), bf16[1024,1,1024]{2,0,1:T(8,128)(2,1)}) %all-gather.18.cloned.1.call-update) | async-done | bytes 2097168 | tf_op jit(solution)/shard_map/while/body/eval_jaxpr/all_gather | solution.py:216
  362.5 7.6 multiply_reduce_fusion.13
  374.6 6.8 multiply_convert_fusion.11
  444.2 11.5 %reduce-scatter.14.cloned.1.call-done = f32[256,1,1024]{2,0,1:T(8,128)} async-done(((f32[1024,1,1024]{2,0,1:T(8,128)}), f32[256,1,1024]{2,0,1:T(8,128)}) %reduce-scatter.14.cloned.1.call-update) | async-done | bytes 1048592 | tf_op jit(solution)/shard_map/while/body/eval_jaxpr/reduce_scatter | solution.py:234
  462.6 22.9 %all-gather.14.cloned.1.call-done = bf16[1024,1,1024]{2,0,1:T(8,128)(2,1)} async-done(((bf16[256,1,1024]{2,0,1:T(8,128)(2,1)}), bf16[1024,1,1024]{2,0,1:T(8,128)(2,1)}) %all-gather.14.cloned.1.call-update) | async-done | bytes 2097168 | tf_op jit(solution)/shard_map/while/body/eval_jaxpr/all_gather | solution.py:155
  507.3 44.7 %reduce-scatter.8.cloned.1.call-done = f32[256,1,1024]{2,0,1:T(8,128)} async-done(((f32[1024,1,1024]{2,0,1:T(8,128)}), f32[256,1,1024]{2,0,1:T(8,128)}) %reduce-scatter.8.cloned.1.call-update) | async-done | bytes 1048592 | tf_op jit(solution)/shard_map/while/body/eval_jaxpr/reduce_scatter | solution.py:169
  555.3 22.2 %all-gather.16.cloned.1.call-done = bf16[1024,1,1024]{2,0,1:T(8,128)(2,1)} async-done(((bf16[256,1,1024]{2,0,1:T(8,128)(2,1)}), bf16[1024,1,1024]{2,0,1:T(8,128)(2,1)}) %all-gather.16.cloned.1.call-update) | async-done | bytes 2097168 | tf_op jit(solution)/shard_map/while/body/eval_jaxpr/all_gather | solution.py:178
  593.7 44.7 %reduce-scatter.12.cloned.1.call-done = f32[256,1,1024]{2,0,1:T(8,128)} async-done(((f32[1024,1,1024]{2,0,1:T(8,128)}), f32[256,1,1024]{2,0,1:T(8,128)}) %reduce-scatter.12.cloned.1.call-update) | async-done | bytes 1048592 | tf_op jit(solution)/shard_map/while/body/eval_jaxpr/reduce_scatter | solution.py:205
  642.9 7.0 convert_bitcast_fusion.4
  650.2 15.4 %all-gather.18.cloned.1.call-done = bf16[1024,1,1024]{2,0,1:T(8,128)(2,1)} async-done(((bf16[256,1,1024]{2,0,1:T(8,128)(2,1)}), bf16[1024,1,1024]{2,0,1:T(8,128)(2,1)}) %all-gather.18.cloned.1.call-update) | async-done | bytes 2097168 | tf_op jit(solution)/shard_map/while/body/eval_jaxpr/all_gather | solution.py:216
  673.0 7.6 multiply_reduce_fusion.13
  685.2 6.8 multiply_convert_fusion.11
  749.2 10.1 maximum_add_fusion.4
  759.3 7.1 reduce-scatter.14.cloned.1.call-done
  774.2 57.3 %all-gather.12.cloned.1.call-done = f32[393216]{0:T(1024)} async-done(((f32[12288]{0:T(1024)}), f32[393216]{0:T(1024)}) %all-gather.12.cloned.1.call-update) | async-done | bytes 1572880 | tf_op jit(solution)/shard_map/all_gather | solution.py:279
  835.2 206.6 %reduce-scatter.6.cloned.1.call-done = f32[128,3072]{0,1:T(8,128)} async-done(((f32[1024,3072]{0,1:T(8,128)}), f32[128,3072]{0,1:T(8,128)}) %reduce-scatter.6.cloned.1.call-update) | async-done | bytes 1572880 | tf_op jit(solution)/shard_map/reduce_scatter | solution.py:267
  (368 shorter events, 280.2 us)
Async XLA Ops:
  7.2 107.7 %all-gather.8.cloned.1.call-start = ((), (), s32[]{:S(2)}) async-start(), calls=%async_computation.5 | async-start | bytes 7077888 | tf_op jit(solution)/shard_map/all_gather | solution.py:125
  12.5 136.6 %all-gather.10.cloned.1.call-start = ((), (), s32[]{:S(2)}) async-start(), calls=%async_computation.6 | async-start | bytes 5242880 | tf_op jit(solution)/shard_map/all_gather | solution.py:131
  122.8 26.3 %copy-start.5 = (bf16[2,256,1,1024]{3,1,2,0:T(8,128)(2,1)S(1)}, bf16[2,256,1,1024]{3,1,2,0:T(8,128)(2,1)}, u32[]{:S(2)}) copy-start(bf16[2,256,1,1024]{3,1,2,0:T(8,128)(2,1)} %param.16) | copy-start | bytes 3145732
  122.8 26.3 %copy-start.20 = (f32[1024]{0:T(1024)S(1)}, f32[1024]{0:T(1024)}, u32[]{:S(2)}) copy-start(f32[1024]{0:T(1024)} %param.25) | copy-start | bytes 12292
  122.8 26.3 %copy-start.21 = (f32[1024]{0:T(1024)S(1)}, f32[1024]{0:T(1024)}, u32[]{:S(2)}) copy-start(f32[1024]{0:T(1024)} %param.27) | copy-start | bytes 12292
  122.8 26.3 %copy-start.22 = (f32[1024]{0:T(1024)S(1)}, f32[1024]{0:T(1024)}, u32[]{:S(2)}) copy-start(f32[1024]{0:T(1024)} %param.26) | copy-start | bytes 12292
  149.4 43.9 %copy-start.16 = (bf16[1024,256]{1,0:T(8,128)(2,1)}, bf16[1024,256]{1,0:T(8,128)(2,1)S(1)}, u32[]{:S(2)}) copy-start(bf16[1024,256]{1,0:T(8,128)(2,1)S(1)} %get-tuple-element.1074) | copy-start | bytes 1572868 | tf_op jit(solution)/shard_map/while
  149.4 25.5 %all-gather.14.cloned.1.call-start = ((), (), s32[]{:S(2)}) async-start(), calls=%async_computation.9 | async-start | bytes 2621440 | tf_op jit(solution)/shard_map/while/body/eval_jaxpr/all_gather | solution.py:155
  151.0 90.4 %reduce-scatter.8.cloned.1.call-start = ((), (), s32[]{:S(2)}) async-start(), calls=%async_computation.10 | async-start | bytes 5242880 | tf_op jit(solution)/shard_map/while/body/eval_jaxpr/reduce_scatter | solution.py:169
  196.7 70.3 %all-gather.16.cloned.1.call-start = ((), (), s32[]{:S(2)}) async-start(), calls=%async_computation.11 | async-start | bytes 2621440 | tf_op jit(solution)/shard_map/while/body/eval_jaxpr/all_gather | solution.py:178
  244.2 83.6 %reduce-scatter.12.cloned.1.call-start = ((), (), s32[]{:S(2)}) async-start(), calls=%async_computation.13 | async-start | bytes 5242880 | tf_op jit(solution)/shard_map/while/body/eval_jaxpr/reduce_scatter | solution.py:205
  283.1 71.9 %all-gather.18.cloned.1.call-start = ((), (), s32[]{:S(2)}) async-start(), calls=%async_computation.14 | async-start | bytes 2621440 | tf_op jit(solution)/shard_map/while/body/eval_jaxpr/all_gather | solution.py:216
  332.2 91.2 %reduce-scatter.10.cloned.1.call-start = ((), (), s32[]{:S(2)}) async-start(), calls=%async_computation.12 | async-start | bytes 2621440 | tf_op jit(solution)/shard_map/while/body/eval_jaxpr/reduce_scatter | solution.py:184
  339.4 116.4 %reduce-scatter.14.cloned.1.call-start = ((), (), s32[]{:S(2)}) async-start(), calls=%async_computation.15 | async-start | bytes 5242880 | tf_op jit(solution)/shard_map/while/body/eval_jaxpr/reduce_scatter | solution.py:234
  460.2 43.6 %copy-start.16 = (bf16[1024,256]{1,0:T(8,128)(2,1)}, bf16[1024,256]{1,0:T(8,128)(2,1)S(1)}, u32[]{:S(2)}) copy-start(bf16[1024,256]{1,0:T(8,128)(2,1)S(1)} %get-tuple-element.1074) | copy-start | bytes 1572868 | tf_op jit(solution)/shard_map/while
  460.2 25.3 %all-gather.14.cloned.1.call-start = ((), (), s32[]{:S(2)}) async-start(), calls=%async_computation.9 | async-start | bytes 2621440 | tf_op jit(solution)/shard_map/while/body/eval_jaxpr/all_gather | solution.py:155
  461.9 90.1 %reduce-scatter.8.cloned.1.call-start = ((), (), s32[]{:S(2)}) async-start(), calls=%async_computation.10 | async-start | bytes 5242880 | tf_op jit(solution)/shard_map/while/body/eval_jaxpr/reduce_scatter | solution.py:169
  507.2 70.3 %all-gather.16.cloned.1.call-start = ((), (), s32[]{:S(2)}) async-start(), calls=%async_computation.11 | async-start | bytes 2621440 | tf_op jit(solution)/shard_map/while/body/eval_jaxpr/all_gather | solution.py:178
  554.8 83.6 %reduce-scatter.12.cloned.1.call-start = ((), (), s32[]{:S(2)}) async-start(), calls=%async_computation.13 | async-start | bytes 5242880 | tf_op jit(solution)/shard_map/while/body/eval_jaxpr/reduce_scatter | solution.py:205
  593.6 71.9 %all-gather.18.cloned.1.call-start = ((), (), s32[]{:S(2)}) async-start(), calls=%async_computation.14 | async-start | bytes 2621440 | tf_op jit(solution)/shard_map/while/body/eval_jaxpr/all_gather | solution.py:216
  642.8 91.3 %reduce-scatter.10.cloned.1.call-start = ((), (), s32[]{:S(2)}) async-start(), calls=%async_computation.12 | async-start | bytes 2621440 | tf_op jit(solution)/shard_map/while/body/eval_jaxpr/reduce_scatter | solution.py:184
  649.9 116.4 %reduce-scatter.14.cloned.1.call-start = ((), (), s32[]{:S(2)}) async-start(), calls=%async_computation.15 | async-start | bytes 5242880 | tf_op jit(solution)/shard_map/while/body/eval_jaxpr/reduce_scatter | solution.py:234
  772.7 58.8 %all-gather.12.cloned.1.call-start = ((), (), s32[]{:S(2)}) async-start(), calls=%async_computation.8 | async-start | bytes 1622016 | tf_op jit(solution)/shard_map/all_gather | solution.py:279
  773.6 268.2 %reduce-scatter.6.cloned.1.call-start = ((), (), s32[]{:S(2)}) async-start(), calls=%async_computation.7 | async-start | bytes 14155776 | tf_op jit(solution)/shard_map/reduce_scatter | solution.py:267
  (64 other events, 451.9 us)
Sparse Core Ops, SparseCore 0:
  12.6 102.1 all-gather.7
  116.4 32.6 all-gather.9
  152.3 22.5 all-gather.13
  196.8 44.5 reduce-scatter.7
  244.3 22.5 all-gather.15
  283.2 44.5 reduce-scatter.11
  332.4 22.5 all-gather.17
  357.5 31.1 reduce-scatter.9
  410.8 44.8 reduce-scatter.13
  462.9 22.5 all-gather.13
  507.3 44.5 reduce-scatter.7
  554.9 22.5 all-gather.15
  593.8 44.5 reduce-scatter.11
  642.9 22.5 all-gather.17
  667.9 31.1 reduce-scatter.9
  721.4 44.8 reduce-scatter.13
  776.6 54.8 all-gather.11
  834.9 206.8 reduce-scatter.5
